TPU v7x, 256 devices: a whole 4x4x8 slice. The times are simulated.
256 devices in a mesh: section: 2 (over z_hi), tile: 64 (over z_lo, y, x), member: 2 (over core).
Axes of the slice: x: 4, y: 4, z: 8 (z_hi: 2, z_lo: 4; z = z_hi * 4 + z_lo), core: 2. Of those that a mesh axis runs over, the one named last changes fastest.
Arguments:
- frames: bfloat16 [2, 128, 128, 8, 128], P(None, ('member', 'tile')), parts along dimension 1, may hold values from -6 to 6
- hidden_init: bfloat16 [4, 128, 128, 8, 128], P('section', ('member', 'tile')), parts along dimension 1, may hold values from -0.8984375 to 0.8984375
- memory_init: float32 [4, 128, 128, 8, 128], P('section', ('member', 'tile')), parts along dimension 1, may hold values from -4 to 4
- weights: bfloat16 [4, 512, 2304], P('section'), may hold values from -0.125 to 0.125
- biases: float32 [4, 512], P('section'), may hold values from -3 to 3
Outputs:
- hidden_out: bfloat16 [4, 128, 128, 8, 128], P('section', ('member', 'tile')), parts along dimension 1
- memory_out: float32 [4, 128, 128, 8, 128], P('section', ('member', 'tile')), parts along dimension 1
- gates_out: bfloat16 [2, 4, 128, 512, 8, 128], P(None, 'section', ('member', 'tile')), parts along dimension 2
There are 2 independent parts, one for each index of `member`. A program takes and returns all parts, laid end to end along the dimension named above; an argument that names none is the same for every part. Nothing has to cross between parts.
All inputs are finite; a program needn't handle non-finite values.
Results may differ from a plain program's by a relative error of at most 0.0021.
Values may be sent and summed in bfloat16 or wider, within the bound.
A program may use at most 128 MiB of HBM per device.

v0:
```python
import jax
import jax.numpy as jnp
from jax import lax
from jax.sharding import PartitionSpec as P

GRID_COLS = 8


def from_behind(block, axis, distance):
    devices = range(lax.axis_size(axis))
    route = [((i - distance) % len(devices), i) for i in devices]
    return lax.ppermute(block, axis, route)


def shifted(shard, axis, by):
    peers = lax.axis_size(axis)
    pairs = [(i, i + by) for i in range(peers) if 0 <= i + by < peers]
    return lax.ppermute(shard, axis, pairs)


def tile_place():
    place = (lax.axis_index("tile") + GRID_COLS + GRID_COLS // 2) % lax.axis_size("tile")
    return (place // GRID_COLS, place % GRID_COLS)


def keep_if(condition, rim):
    return jnp.where(condition, rim, jnp.zeros_like(rim))


def with_rims(source_field):
    row_place, column_place = tile_place()
    grid_rows = lax.axis_size("tile") // GRID_COLS
    upper_rim = from_behind(source_field[:, -1:, :], "tile", GRID_COLS)
    lower_rim = from_behind(source_field[:, :1, :], "tile", -GRID_COLS)
    upper_rim = keep_if(row_place > 0, upper_rim)
    lower_rim = keep_if(row_place < grid_rows - 1, lower_rim)
    heightened = jnp.concatenate([upper_rim, source_field, lower_rim], axis=1)
    left_rim = from_behind(heightened[:, :, -1:], "tile", 1)
    right_rim = from_behind(heightened[:, :, :1], "tile", -1)
    left_rim = keep_if(column_place > 0, left_rim)
    right_rim = keep_if(column_place < GRID_COLS - 1, right_rim)
    return jnp.concatenate([left_rim, heightened, right_rim], axis=2)


def hand_over(hidden_state):
    return shifted(hidden_state, "section", 1)


def advance(stacked, layer_weights, bias_row, memory):
    hidden_count = memory.shape[0]
    height = stacked.shape[1] - 2
    breadth = stacked.shape[2] - 2
    shifted_views = [
        stacked[:, row_offset : row_offset + height, column_offset : column_offset + breadth]
        for row_offset in range(3)
        for column_offset in range(3)
    ]
    patches = jnp.concatenate(shifted_views, axis=0).reshape(9 * stacked.shape[0], height * breadth)
    preact = jnp.dot(layer_weights, patches, preferred_element_type=jnp.float32) + bias_row[:, None]
    preact = preact.reshape(4, hidden_count, height, breadth)
    inflow = jax.nn.sigmoid(preact[0])
    forget = jax.nn.sigmoid(preact[1])
    outflow = jax.nn.sigmoid(preact[2])
    candidate = jnp.tanh(preact[3])
    memory = forget * memory + inflow * candidate
    hidden_state = (outflow * jnp.tanh(memory)).astype(jnp.bfloat16)
    opened = (
        jnp.stack([inflow, forget, outflow, candidate])
        .reshape(4 * hidden_count, height, breadth)
        .astype(jnp.bfloat16)
    )
    return (hidden_state, memory, opened)


def body(frames, hidden_init, memory_init, weights, biases):
    step_count = frames.shape[0]
    layer_count = weights.shape[0]
    channels = frames.shape[2]
    first_section = lax.axis_index("section") == 0
    saved_gates = []
    states = [hidden_init[layer_index, 0] for layer_index in range(layer_count)]
    memories = [memory_init[layer_index, 0] for layer_index in range(layer_count)]
    for moment in range(step_count):
        received = hand_over(states[-1])
        incoming = jnp.where(first_section, frames[moment, 0], received)
        padded = with_rims(jnp.concatenate([incoming] + states, axis=0))
        layer_stacks = [
            padded[layer_index * channels : (layer_index + 2) * channels]
            for layer_index in range(layer_count)
        ]
        fresh_states = []
        fresh_memories = []
        opened_step = []
        for layer_index in range(layer_count):
            hidden_state, memory, opened = advance(
                layer_stacks[layer_index],
                weights[layer_index],
                biases[layer_index],
                memories[layer_index],
            )
            fresh_states.append(hidden_state)
            fresh_memories.append(memory)
            opened_step.append(opened)
        states = fresh_states
        memories = fresh_memories
        saved_gates.append(jnp.stack(opened_step))
    hidden_out = jnp.stack(states)[:, None]
    memory_out = jnp.stack(memories)[:, None]
    gates_out = jnp.stack(saved_gates)[:, :, None]
    return (hidden_out, memory_out, gates_out)


def solution(mesh):
    in_specs = (
        P(None, ("member", "tile"), None, None, None),
        P("section", ("member", "tile"), None, None, None),
        P("section", ("member", "tile"), None, None, None),
        P("section", None, None),
        P("section", None),
    )
    out_specs = (
        P("section", ("member", "tile"), None, None, None),
        P("section", ("member", "tile"), None, None, None),
        P(None, "section", ("member", "tile"), None, None, None),
    )
    return jax.shard_map(body, mesh=mesh, in_specs=in_specs, out_specs=out_specs, check_vma=False)
```

profile of v0, /device:TPU:128, one launch (start us, length us, event | category | flops | bytes accessed | tf_op | source)
XLA Modules:
  0.0 122.2 jit_solution(7651265513706469046)
XLA Ops:
  6.1 9.8 %collective-permute-done = bf16[128,8,128]{0,2,1:T(8,128)(2,1)S(1)} collective-permute-done((bf16[128,8,128]{0,2,1:T(8,128)(2,1)S(1)}, bf16[128,8,128]{0,2,1:T(8,128)(2,1)S(1)}, u32[]{:S(2)}, u32[]{:S(2)}) %collective-permute-start) | collective-permute-done | bytes 262176 | tf_op jit(solution)/shard_map/ppermute | solution.py:18
  16.0 4.6 %collective-permute-start.2 = (bf16[384,1,128]{0,2,1:T(8,128)(2,1)S(1)}, bf16[384,1,128]{0,2,1:T(8,128)(2,1)S(1)}, u32[]{:S(2)}, u32[]{:S(2)}) collective-permute-start(bf16[384,1,128]{0,2,1:T(8,128)(2,1)S(1)} %get-tuple-element.91), channel_id=1, source_target_pairs={{16,0},{18,2},{20,4},{22,6},{24,8},{26,10},{28,12},{30,14},{32,16}... | collective-permute-start | bytes 294920 | tf_op jit(solution)/shard_map/ppermute | solution.py:12
  22.8 8.0 %collective-permute-done.1 = bf16[384,1,128]{0,2,1:T(8,128)(2,1)S(1)} collective-permute-done((bf16[384,1,128]{0,2,1:T(8,128)(2,1)S(1)}, bf16[384,1,128]{0,2,1:T(8,128)(2,1)S(1)}, u32[]{:S(2)}, u32[]{:S(2)}) %collective-permute-start.1) | collective-permute-done | bytes 98336 | tf_op jit(solution)/shard_map/ppermute | solution.py:12
  31.1 5.4 %collective-permute-start.4 = (bf16[384,10,1]{0,1,2:T(8,128)(2,1)S(1)}, bf16[384,10,1]{0,1,2:T(8,128)(2,1)S(1)}, u32[]{:S(2)}, u32[]{:S(2)}) collective-permute-start(bf16[384,10,1]{0,1,2:T(8,128)(2,1)S(1)} %copy.98), channel_id=1, source_target_pairs={{2,0},{4,2},{6,4},{8,6},{10,8},{12,10},{14,12},{16,14},{18,16},{20... | collective-permute-start | bytes 23048 | tf_op jit(solution)/shard_map/ppermute | solution.py:12
  37.9 8.3 %collective-permute-done.3 = bf16[384,10,1]{0,1,2:T(8,128)(2,1)S(1)} collective-permute-done((bf16[384,10,1]{0,1,2:T(8,128)(2,1)S(1)}, bf16[384,10,1]{0,1,2:T(8,128)(2,1)S(1)}, u32[]{:S(2)}, u32[]{:S(2)}) %collective-permute-start.3) | collective-permute-done | bytes 7712 | tf_op jit(solution)/shard_map/ppermute | solution.py:12
  49.5 1.5 %slice-done.1 = s8[4194304]{0:T(1024)(128)(4,1)S(1)} async-done(((s8[4718592]{0:T(1024)(128)(4,1)}), s8[4194304]{0:T(1024)(128)(4,1)S(1)}, s32[]{:S(2)}) %slice-start.1) | async-done | bytes 4194328
  51.0 2.6 %add_bitcast_fusion.3 = f32[512,1024]{0,1:T(8,128)S(1)} fusion(bf16[2304,1024]{0,1:T(8,128)(2,1)S(1)} %constant_dynamic-update-slice_fusion, bf16[2,512,2304]{2,1,0:T(8,128)(2,1)S(1)} %bitcast.210, f32[512]{0:T(512)S(1)} %bitcast.207), kind=kOutput, calls=%fused_computation.14 | convolution fusion | flops 2416443392 | bytes 9177088 | tf_op jit(solution)/shard_map/dot_general | solution.py:59
  54.3 2.6 %add_bitcast_fusion.2 = f32[512,1024]{0,1:T(8,128)S(1)} fusion(bf16[2304,1024]{0,1:T(8,128)(2,1)S(1)} %constant_dynamic-update-slice_fusion.10, bf16[2,512,2304]{2,1,0:T(8,128)(2,1)S(1)} %bitcast.210, f32[512]{0:T(512)S(1)} %bitcast.205), kind=kOutput, calls=%fused_computation.13 | convolution fusion | flops 2416443392 | bytes 9177088 | tf_op jit(solution)/shard_map/dot_general | solution.py:59
  57.0 1.5 %fusion.79 = (bf16[128,1024]{0,1:T(8,128)(2,1)}, bf16[128,1024]{0,1:T(8,128)(2,1)}, f32[128,1024]{0,1:T(8,128)S(1)}, f32[128,1024]{0,1:T(8,128)S(1)}, bf16[128,1024]{0,1:T(8,128)(2,1)}, /*index=5*/f32[128,1024]{0,1:T(8,128)}) fusion(f32[512,1024]{0,1:T(8,128)S(1)} %add_bitcast_fusion.2), kind=kLoop, calls=%fused_computation.142 | loop fusion | flops 1703936 | bytes 4456448 | tf_op jit(solution)/shard_map/convert.13
  58.6 1.5 %collective-permute-start.5 = (bf16[128,8,128]{0,2,1:T(8,128)(2,1)S(1)}, bf16[128,8,128]{0,2,1:T(8,128)(2,1)}, u32[]{:S(2)}, u32[]{:S(2)}) collective-permute-start(bf16[128,8,128]{0,2,1:T(8,128)(2,1)S(1)} %fusion.69), channel_id=1, source_target_pairs={{0,128},{1,129},{2,130},{3,131},{4,132},{5,133},{6,134},{7,135},{8... | collective-permute-start | bytes 786440 | tf_op jit(solution)/shard_map/ppermute | solution.py:18
  60.3 1.5 %copy.107 = bf16[4,128,8,128]{3,2,1,0:T(8,128)(2,1)} copy(bf16[4,128,8,128]{1,3,2,0:T(8,128)(2,1)S(1)} %pad_maximum_fusion.1) | data formatting | bytes 2097152 | tf_op jit(solution)/shard_map/stack | solution.py:68
  63.0 1.5 %copy.106 = bf16[4,128,8,128]{3,2,1,0:T(8,128)(2,1)} copy(bf16[4,128,8,128]{1,3,2,0:T(8,128)(2,1)S(1)} %pad_maximum_fusion) | data formatting | bytes 2097152 | tf_op jit(solution)/shard_map/stack | solution.py:68
  65.8 5.2 %collective-permute-done.5 = bf16[128,8,128]{0,2,1:T(8,128)(2,1)} collective-permute-done((bf16[128,8,128]{0,2,1:T(8,128)(2,1)S(1)}, bf16[128,8,128]{0,2,1:T(8,128)(2,1)}, u32[]{:S(2)}, u32[]{:S(2)}) %collective-permute-start.5) | collective-permute-done | bytes 262176 | tf_op jit(solution)/shard_map/ppermute | solution.py:18
  72.4 3.6 %collective-permute-start.6 = (bf16[384,1,128]{0,2,1:T(8,128)(2,1)S(1)}, bf16[384,1,128]{0,2,1:T(8,128)(2,1)S(1)}, u32[]{:S(2)}, u32[]{:S(2)}) collective-permute-start(bf16[384,1,128]{0,2,1:T(8,128)(2,1)S(1)} %get-tuple-element.86), channel_id=1, source_target_pairs={{112,0},{114,2},{116,4},{118,6},{120,8},{122,10},{124,12},{126,14}... | collective-permute-start | bytes 294920 | tf_op jit(solution)/shard_map/ppermute | solution.py:12
  76.0 2.3 %collective-permute-done.7 = bf16[384,1,128]{0,2,1:T(8,128)(2,1)S(1)} collective-permute-done((bf16[384,1,128]{0,2,1:T(8,128)(2,1)S(1)}, bf16[384,1,128]{0,2,1:T(8,128)(2,1)S(1)}, u32[]{:S(2)}, u32[]{:S(2)}) %collective-permute-start.7) | collective-permute-done | bytes 98336 | tf_op jit(solution)/shard_map/ppermute | solution.py:12
  78.3 3.0 %collective-permute-done.6 = bf16[384,1,128]{0,2,1:T(8,128)(2,1)S(1)} collective-permute-done((bf16[384,1,128]{0,2,1:T(8,128)(2,1)S(1)}, bf16[384,1,128]{0,2,1:T(8,128)(2,1)S(1)}, u32[]{:S(2)}, u32[]{:S(2)}) %collective-permute-start.6) | collective-permute-done | bytes 98336 | tf_op jit(solution)/shard_map/ppermute | solution.py:12
  82.1 1.7 %collective-permute-start.8 = (bf16[384,10,1]{0,1,2:T(8,128)(2,1)S(1)}, bf16[384,10,1]{0,1,2:T(8,128)(2,1)S(1)}, u32[]{:S(2)}, u32[]{:S(2)}) collective-permute-start(bf16[384,10,1]{0,1,2:T(8,128)(2,1)S(1)} %copy.102), channel_id=1, source_target_pairs={{126,0},{0,2},{2,4},{4,6},{6,8},{8,10},{10,12},{12,14},{14,16},{16... | collective-permute-start | bytes 23048 | tf_op jit(solution)/shard_map/ppermute | solution.py:12
  85.2 6.7 %collective-permute-done.8 = bf16[384,10,1]{0,1,2:T(8,128)(2,1)S(1)} collective-permute-done((bf16[384,10,1]{0,1,2:T(8,128)(2,1)S(1)}, bf16[384,10,1]{0,1,2:T(8,128)(2,1)S(1)}, u32[]{:S(2)}, u32[]{:S(2)}) %collective-permute-start.8) | collective-permute-done | bytes 7712 | tf_op jit(solution)/shard_map/ppermute | solution.py:12
  96.0 2.6 %add_bitcast_fusion = f32[512,1024]{0,1:T(8,128)S(1)} fusion(bf16[2304,1024]{0,1:T(8,128)(2,1)S(1)} %bitcast.204, bf16[2,512,2304]{2,1,0:T(8,128)(2,1)S(1)} %bitcast.212, f32[512]{0:T(512)S(1)} %bitcast.208), kind=kOutput, calls=%fused_computation.11 | convolution fusion | flops 2416443392 | bytes 9177088 | tf_op jit(solution)/shard_map/dot_general | solution.py:59
  99.9 2.6 %add_bitcast_fusion.1 = f32[512,1024]{0,1:T(8,128)S(1)} fusion(bf16[2304,1024]{0,1:T(8,128)(2,1)S(1)} %bitcast.203, bf16[2,512,2304]{2,1,0:T(8,128)(2,1)S(1)} %bitcast.212, f32[512]{0:T(512)S(1)} %bitcast.206), kind=kOutput, calls=%fused_computation.12 | convolution fusion | flops 2416443392 | bytes 9177088 | tf_op jit(solution)/shard_map/dot_general | solution.py:59
  113.9 1.5 %copy.109 = bf16[4,128,8,128]{3,2,1,0:T(8,128)(2,1)} copy(bf16[4,128,8,128]{1,3,2,0:T(8,128)(2,1)S(1)} %pad_maximum_fusion.3) | data formatting | bytes 2097152 | tf_op jit(solution)/shard_map/stack | solution.py:68
  116.6 1.5 %copy.108 = bf16[4,128,8,128]{3,2,1,0:T(8,128)(2,1)} copy(bf16[4,128,8,128]{1,3,2,0:T(8,128)(2,1)S(1)} %pad_maximum_fusion.2) | data formatting | bytes 2097152 | tf_op jit(solution)/shard_map/stack | solution.py:68
  118.1 1.7 %maximum_bitcast_fusion.2 = bf16[1,2,512,8,128]{4,3,2,1,0:T(8,128)(2,1)S(1)} fusion(bf16[1,512,8,128]{3,2,1,0:T(8,128)(2,1)} %bitcast.171, bf16[1,512,8,128]{3,2,1,0:T(8,128)(2,1)} %bitcast.172), kind=kLoop, calls=%fused_computation.10 | loop fusion | flops 1048576 | bytes 4194304 | tf_op jit(solution)/shard_map/stack | solution.py:109
  119.8 2.4 %maximum_bitcast_fusion = bf16[2,2,1,512,8,128]{5,4,3,2,1,0:T(8,128)(2,1)} fusion(bf16[1,2,512,8,128]{4,3,2,1,0:T(8,128)(2,1)S(1)} %maximum_bitcast_fusion.2, bf16[1,2,512,8,128]{4,3,2,1,0:T(8,128)(2,1)S(1)} %maximum_bitcast_fusion.1), kind=kLoop, calls=%fused_computation | loop fusion | flops 2097152 | bytes 8388608
  (131 shorter events, 37.5 us)
Async XLA Ops:
  0.6 20.0 %copy-start.11 = (f32[2,512]{1,0:T(2,128)S(1)}, f32[2,512]{1,0:T(2,128)}, u32[]{:S(2)}) copy-start(f32[2,512]{1,0:T(2,128)} %param.9) | copy-start | bytes 12292
  1.9 13.9 %collective-permute-start = (bf16[128,8,128]{0,2,1:T(8,128)(2,1)S(1)}, bf16[128,8,128]{0,2,1:T(8,128)(2,1)S(1)}, u32[]{:S(2)}, u32[]{:S(2)}) collective-permute-start(bf16[128,8,128]{0,2,1:T(8,128)(2,1)S(1)} %bitcast.139), channel_id=1, source_target_pairs={{0,128},{1,129},{2,130},{3,131},{4,132},{5,133},{6,134},{7,135},{8... | collective-permute-start | bytes 786440 | tf_op jit(solution)/shard_map/ppermute | solution.py:18
  16.0 6.8 %collective-permute-start.2 = (bf16[384,1,128]{0,2,1:T(8,128)(2,1)S(1)}, bf16[384,1,128]{0,2,1:T(8,128)(2,1)S(1)}, u32[]{:S(2)}, u32[]{:S(2)}) collective-permute-start(bf16[384,1,128]{0,2,1:T(8,128)(2,1)S(1)} %get-tuple-element.91), channel_id=1, source_target_pairs={{16,0},{18,2},{20,4},{22,6},{24,8},{26,10},{28,12},{30,14},{32,16}... | collective-permute-start | bytes 294920 | tf_op jit(solution)/shard_map/ppermute | solution.py:12
  20.8 37.6 %copy-start.6 = (f32[1,1,128,8,128]{2,4,3,1,0:T(8,128)}, f32[1,1,128,8,128]{2,4,3,1,0:T(8,128)S(1)}, u32[]{:S(2)}) copy-start(f32[1,1,128,8,128]{2,4,3,1,0:T(8,128)S(1)} %copy.117) | copy-start | bytes 1572868
  21.1 43.4 %copy-start.4 = (f32[1,1,128,8,128]{2,4,3,1,0:T(8,128)}, f32[1,1,128,8,128]{2,4,3,1,0:T(8,128)S(1)}, u32[]{:S(2)}) copy-start(f32[1,1,128,8,128]{2,4,3,1,0:T(8,128)S(1)} %copy.118) | copy-start | bytes 1572868
  22.0 8.8 %collective-permute-start.1 = (bf16[384,1,128]{0,2,1:T(8,128)(2,1)S(1)}, bf16[384,1,128]{0,2,1:T(8,128)(2,1)S(1)}, u32[]{:S(2)}, u32[]{:S(2)}) collective-permute-start(bf16[384,1,128]{0,2,1:T(8,128)(2,1)S(1)} %get-tuple-element.90), channel_id=1, source_target_pairs={{112,0},{114,2},{116,4},{118,6},{120,8},{122,10},{124,12},{126,14}... | collective-permute-start | bytes 294920 | tf_op jit(solution)/shard_map/ppermute | solution.py:12
  31.1 6.8 %collective-permute-start.4 = (bf16[384,10,1]{0,1,2:T(8,128)(2,1)S(1)}, bf16[384,10,1]{0,1,2:T(8,128)(2,1)S(1)}, u32[]{:S(2)}, u32[]{:S(2)}) collective-permute-start(bf16[384,10,1]{0,1,2:T(8,128)(2,1)S(1)} %copy.98), channel_id=1, source_target_pairs={{2,0},{4,2},{6,4},{8,6},{10,8},{12,10},{14,12},{16,14},{18,16},{20... | collective-permute-start | bytes 23048 | tf_op jit(solution)/shard_map/ppermute | solution.py:12
  36.4 9.7 %collective-permute-start.3 = (bf16[384,10,1]{0,1,2:T(8,128)(2,1)S(1)}, bf16[384,10,1]{0,1,2:T(8,128)(2,1)S(1)}, u32[]{:S(2)}, u32[]{:S(2)}) collective-permute-start(bf16[384,10,1]{0,1,2:T(8,128)(2,1)S(1)} %copy.96), channel_id=1, source_target_pairs={{126,0},{0,2},{2,4},{4,6},{6,8},{8,10},{10,12},{12,14},{14,16},{16... | collective-permute-start | bytes 23048 | tf_op jit(solution)/shard_map/ppermute | solution.py:12
  48.8 2.2 %slice-start.1 = ((s8[4718592]{0:T(1024)(128)(4,1)}), s8[4194304]{0:T(1024)(128)(4,1)S(1)}, s32[]{:S(2)}) async-start(s8[4718592]{0:T(1024)(128)(4,1)} %bitcast.209), calls=%async_computation.1 | async-start | bytes 8388608
  54.1 4.3 %copy-start = (f32[128,1024]{0,1:T(8,128)}, f32[128,1024]{0,1:T(8,128)S(1)}, u32[]{:S(2)}) copy-start(f32[128,1024]{0,1:T(8,128)S(1)} %get-tuple-element.28) | copy-start | bytes 1572868
  58.4 6.1 %copy-start.2 = (f32[128,1024]{0,1:T(8,128)}, f32[128,1024]{0,1:T(8,128)S(1)}, u32[]{:S(2)}) copy-start(f32[128,1024]{0,1:T(8,128)S(1)} %get-tuple-element.22) | copy-start | bytes 1572868
  58.6 12.4 %collective-permute-start.5 = (bf16[128,8,128]{0,2,1:T(8,128)(2,1)S(1)}, bf16[128,8,128]{0,2,1:T(8,128)(2,1)}, u32[]{:S(2)}, u32[]{:S(2)}) collective-permute-start(bf16[128,8,128]{0,2,1:T(8,128)(2,1)S(1)} %fusion.69), channel_id=1, source_target_pairs={{0,128},{1,129},{2,130},{3,131},{4,132},{5,133},{6,134},{7,135},{8... | collective-permute-start | bytes 786440 | tf_op jit(solution)/shard_map/ppermute | solution.py:18
  64.5 7.7 %copy-start.8 = (bf16[4,128,8,128]{3,2,1,0:T(8,128)(2,1)S(1)}, bf16[4,128,8,128]{3,2,1,0:T(8,128)(2,1)}, u32[]{:S(2)}) copy-start(bf16[4,128,8,128]{3,2,1,0:T(8,128)(2,1)} %copy.107) | copy-start | bytes 3145732
  64.5 7.7 %copy-start.9 = (bf16[4,128,8,128]{3,2,1,0:T(8,128)(2,1)S(1)}, bf16[4,128,8,128]{3,2,1,0:T(8,128)(2,1)}, u32[]{:S(2)}) copy-start(bf16[4,128,8,128]{3,2,1,0:T(8,128)(2,1)} %copy.106) | copy-start | bytes 3145732
  72.1 6.2 %collective-permute-start.7 = (bf16[384,1,128]{0,2,1:T(8,128)(2,1)S(1)}, bf16[384,1,128]{0,2,1:T(8,128)(2,1)S(1)}, u32[]{:S(2)}, u32[]{:S(2)}) collective-permute-start(bf16[384,1,128]{0,2,1:T(8,128)(2,1)S(1)} %get-tuple-element.87), channel_id=1, source_target_pairs={{16,0},{18,2},{20,4},{22,6},{24,8},{26,10},{28,12},{30,14},{32,16}... | collective-permute-start | bytes 294920 | tf_op jit(solution)/shard_map/ppermute | solution.py:12
  72.4 8.9 %collective-permute-start.6 = (bf16[384,1,128]{0,2,1:T(8,128)(2,1)S(1)}, bf16[384,1,128]{0,2,1:T(8,128)(2,1)S(1)}, u32[]{:S(2)}, u32[]{:S(2)}) collective-permute-start(bf16[384,1,128]{0,2,1:T(8,128)(2,1)S(1)} %get-tuple-element.86), channel_id=1, source_target_pairs={{112,0},{114,2},{116,4},{118,6},{120,8},{122,10},{124,12},{126,14}... | collective-permute-start | bytes 294920 | tf_op jit(solution)/shard_map/ppermute | solution.py:12
  81.4 3.8 %collective-permute-start.9 = (bf16[384,10,1]{0,1,2:T(8,128)(2,1)S(1)}, bf16[384,10,1]{0,1,2:T(8,128)(2,1)S(1)}, u32[]{:S(2)}, u32[]{:S(2)}) collective-permute-start(bf16[384,10,1]{0,1,2:T(8,128)(2,1)S(1)} %copy.104), channel_id=1, source_target_pairs={{2,0},{4,2},{6,4},{8,6},{10,8},{12,10},{14,12},{16,14},{18,16},{20... | collective-permute-start | bytes 23048 | tf_op jit(solution)/shard_map/ppermute | solution.py:12
  82.1 9.8 %collective-permute-start.8 = (bf16[384,10,1]{0,1,2:T(8,128)(2,1)S(1)}, bf16[384,10,1]{0,1,2:T(8,128)(2,1)S(1)}, u32[]{:S(2)}, u32[]{:S(2)}) collective-permute-start(bf16[384,10,1]{0,1,2:T(8,128)(2,1)S(1)} %copy.102), channel_id=1, source_target_pairs={{126,0},{0,2},{2,4},{4,6},{6,8},{8,10},{10,12},{12,14},{14,16},{16... | collective-permute-start | bytes 23048 | tf_op jit(solution)/shard_map/ppermute | solution.py:12
  93.5 2.2 %slice-start.2 = ((s8[4718592]{0:T(1024)(128)(4,1)}), s8[4194304]{0:T(1024)(128)(4,1)S(1)}, s32[]{:S(2)}) async-start(s8[4718592]{0:T(1024)(128)(4,1)} %bitcast.211), calls=%async_computation.2 | async-start | bytes 8388608
  102.5 4.3 %copy-start.1 = (f32[128,1024]{0,1:T(8,128)S(1)}, f32[128,1024]{0,1:T(8,128)}, u32[]{:S(2)}) copy-start(f32[128,1024]{0,1:T(8,128)} %copy-done) | copy-start | bytes 1572868
  102.6 4.3 %copy-start.7 = (f32[1,1,128,8,128]{2,4,3,1,0:T(8,128)S(1)}, f32[1,1,128,8,128]{2,4,3,1,0:T(8,128)}, u32[]{:S(2)}) copy-start(f32[1,1,128,8,128]{2,4,3,1,0:T(8,128)} %copy-done.6) | copy-start | bytes 1572868
  102.6 5.3 %copy-start.3 = (f32[128,1024]{0,1:T(8,128)S(1)}, f32[128,1024]{0,1:T(8,128)}, u32[]{:S(2)}) copy-start(f32[128,1024]{0,1:T(8,128)} %copy-done.2) | copy-start | bytes 1572868
  102.6 5.3 %copy-start.5 = (f32[1,1,128,8,128]{2,4,3,1,0:T(8,128)S(1)}, f32[1,1,128,8,128]{2,4,3,1,0:T(8,128)}, u32[]{:S(2)}) copy-start(f32[1,1,128,8,128]{2,4,3,1,0:T(8,128)} %copy-done.4) | copy-start | bytes 1572868
  108.9 3.7 %copy-start.10 = (bf16[128,1024]{0,1:T(8,128)(2,1)S(1)}, bf16[128,1024]{0,1:T(8,128)(2,1)}, u32[]{:S(2)}) copy-start(bf16[128,1024]{0,1:T(8,128)(2,1)} %get-tuple-element.37) | copy-start | bytes 786436
  (2 other events, 2.7 us)
where the time goes:
time: 124 us; the launch traced here: 122 us
  waiting for transfers between devices  46.7 us (38%)
  other arithmetic  25 us (20%)
  local copies, waits for them, and re-layouts  20.1 us (16%)
  starting transfers between devices  18.6 us (15%)
  matrix products  10.5 us (8%)
  between operations  1.32 us (1%)
    ppermute x8, waiting for transfers between devices, from_behind(): return lax.ppermute(block, axis, route)  31.7 us
    ppermute x8, starting transfers between devices, from_behind(): return lax.ppermute(block, axis, route)  15.8 us
    ppermute x2, waiting for transfers between devices, shifted(): return lax.ppermute(shard, axis, pairs)  15 us
    dot_general x4, matrix products, advance(): jnp.dot(layer_weights, patches, preferred_element_type=jnp.float32)  10.5 us
    unnamed x67, local copies, waits for them, and re-layouts  9.28 us
    another operation x10, other arithmetic  7.61 us
    another operation x4, local copies, waits for them, and re-layouts, advance(): jnp.stack([inflow, forget, outflow, candidate])  5.82 us
    another operation x4, other arithmetic, advance(): jnp.stack([inflow, forget, outflow, candidate])  3.93 us
  transfers between devices with their start and end apart: 10, of which 10 were waited for; matrix products, arithmetic and copies ran while one was open for 9% of the time, Pallas kernels for 0%

commit v1 on v0

v1 whole, which is shorter than its diff:
```python
import jax
import jax.numpy as jnp
from jax import lax
from jax.experimental import pallas as pl
from jax.experimental.pallas import tpu as pltpu
from jax.sharding import PartitionSpec as P

GRID_COLS = 8
MESH = pl.DeviceIdType.MESH
F32 = jnp.float32
BF16 = jnp.bfloat16

ROW_UP, ROW_DOWN = 0, 1
NEIGHBOURS = (-8, 8, 1, 9, -7, -1, 7, -9)
BULK = 2


def sigmoid(x):
    return 0.5 * jnp.tanh(0.5 * x) + 0.5


def kernel(
    frames, hidden, memory, weights, biases,
    hidden_out, memory_out, gates_out,
    patch, spread, hidden_raw, frames_raw, cell, weight, bias_rows, bias,
    gate_wide, gate_narrow, hidden_narrow, edge_send, edge_recv,
    load_sem, store_sem, send_sem, recv_sem, bulk_send, bulk_recv,
):
    section = lax.axis_index("section")
    tile = lax.axis_index("tile")
    member = lax.axis_index("member")
    tiles = lax.axis_size("tile")
    place = lax.rem(tile + GRID_COLS + GRID_COLS // 2, tiles)
    grid_row, grid_col = place // GRID_COLS, lax.rem(place, GRID_COLS)
    has_up, has_down = grid_row > 0, grid_row < tiles // GRID_COLS - 1
    has_left, has_right = grid_col > 0, grid_col < GRID_COLS - 1

    def device(which, distance):
        return (which, lax.rem(tile + distance + tiles, tiles), member)

    loads = [
        pltpu.make_async_copy(hidden, hidden_raw, load_sem.at[0]),
        pltpu.make_async_copy(frames, frames_raw, load_sem.at[1]),
        pltpu.make_async_copy(biases, bias_rows, load_sem.at[2]),
        pltpu.make_async_copy(weights.at[1], weight.at[1], load_sem.at[3]),
        pltpu.make_async_copy(memory, cell, load_sem.at[4]),
        pltpu.make_async_copy(weights.at[0], weight.at[0], load_sem.at[5]),
    ]
    for load in loads:
        load.start()

    barrier = pltpu.get_barrier_semaphore()
    for distance in NEIGHBOURS:
        pl.semaphore_signal(barrier, 1, device_id=device(section, distance), device_id_type=MESH)
    for distance in (0,) + NEIGHBOURS:
        pl.semaphore_signal(barrier, 1, device_id=device(1 - section, distance), device_id_type=MESH)

    def slot(index):
        return pl.ds(index * 128, 128)

    def message(step, source, target, flow, which, number):
        if number == ROW_UP:
            src = patch.at[step, 1, 1, slot(source)]
            dst = patch.at[step, 1, 9, slot(target)]
        elif number == ROW_DOWN:
            src = patch.at[step, 1, 8, slot(source)]
            dst = patch.at[step, 1, 0, slot(target)]
        else:
            src = edge_send.at[step, source, 0 if number < 5 else 1]
            dst = edge_recv.at[step, target, number - 2]
        return pltpu.make_async_remote_copy(
            src_ref=src, dst_ref=dst,
            send_sem=send_sem.at[step, flow, number], recv_sem=recv_sem.at[step, target, number],
            device_id=device(which, NEIGHBOURS[number]), device_id_type=MESH,
        )

    def messages(step, source, target, flow, which):
        return [message(step, source, target, flow, which, n) for n in range(8)]

    def bulk(step):
        rows = 8 // BULK
        return [
            pltpu.make_async_remote_copy(
                src_ref=patch.at[step, 1, pl.ds(1 + n * rows, rows), slot(2)],
                dst_ref=patch.at[step, 1, pl.ds(1 + n * rows, rows), slot(0)],
                send_sem=bulk_send.at[step, n], recv_sem=bulk_recv.at[step, n],
                device_id=device(1, 0), device_id_type=MESH,
            )
            for n in range(BULK)
        ]

    def lay_out(raw, step, index):
        spread[...] = raw.astype(F32)
        for y in range(8):
            patch[step, 1, 1 + y, slot(index), :] = spread[pl.ds(y, 128, stride=8), :].astype(BF16)

    row_of = lax.broadcasted_iota(jnp.int32, (16, 128), 0)
    lane_of = lax.broadcasted_iota(jnp.int32, (16, 128), 1)

    def take_edges(step, index):
        left = jnp.zeros((16, 128), F32)
        right = jnp.zeros((16, 128), F32)
        for y in range(8):
            pick = jnp.concatenate(
                [((row_of == y) & (lane_of == 0)).astype(F32), ((row_of == y) & (lane_of == 127)).astype(F32)], axis=0
            ).astype(BF16)
            both = lax.dot_general(
                pick, patch[step, 1, 1 + y, slot(index), :], (((1,), (1,)), ((), ())), preferred_element_type=F32
            )
            left += both[:16]
            right += both[16:]
        edge_send[step, index, 0] = right.astype(BF16)
        edge_send[step, index, 1] = left.astype(BF16)

    lane = lax.broadcasted_iota(jnp.int32, (128, 128), 1)

    def insert(step, index):
        edges = edge_recv[step, index].reshape(96, 128).astype(F32)
        edges = jnp.concatenate([edges, jnp.zeros((32, 128), F32)], axis=0).T

        def one_row(r, left_at, right_at, live):
            x = patch[step, 1, r, slot(index), :].astype(F32)
            if live is not None:
                x = jnp.where(live, x, 0.0)
                patch[step, 1, r, slot(index), :] = x.astype(BF16)
            from_left = jnp.where(has_left if live is None else live & has_left, pltpu.roll(edges, 128 - left_at, 1), 0.0)
            from_right = jnp.where(has_right if live is None else live & has_right, pltpu.roll(edges, 127 - right_at, 1), 0.0)
            patch[step, 0, r, slot(index), :] = jnp.where(lane == 0, from_left, pltpu.roll(x, 1, 1)).astype(BF16)
            patch[step, 2, r, slot(index), :] = jnp.where(lane == 127, from_right, pltpu.roll(x, 127, 1)).astype(BF16)

        def inner_row(r, carry):
            one_row(r, r - 1, r + 47, None)
            return carry

        one_row(0, 23, 71, has_up)
        one_row(9, 32, 80, has_down)
        lax.fori_loop(1, 9, inner_row, 0)

    def layer(step, index):
        width = pl.ds(index * 128, 256)

        def two_rows(pair, carry):
            acc = None
            for a in range(3):
                for b in range(3):
                    rhs = jnp.concatenate(
                        [patch[step, b, 2 * pair + r + a, width, :] for r in range(2)], axis=1
                    )
                    tap = a * 3 + b
                    part = jnp.dot(weight[index, :, tap * 256:(tap + 1) * 256], rhs, preferred_element_type=F32)
                    acc = part if acc is None else acc + part
            for r in range(2):
                y = 2 * pair + r
                pre = acc[:, r * 128:(r + 1) * 128] + bias[index]
                inflow = sigmoid(pre[0:128])
                forget = sigmoid(pre[128:256])
                outflow = sigmoid(pre[256:384])
                candidate = jnp.tanh(pre[384:512])
                for n, gate in enumerate((inflow, forget, outflow, candidate)):
                    gate_wide[pl.ds(y + n * 1024, 128, stride=8), :] = gate
                old = cell[index, pl.ds(y, 128, stride=8), :]
                new = forget * old + inflow * candidate
                cell[index, pl.ds(y, 128, stride=8), :] = new
                state = outflow * jnp.tanh(new)
                if step == 0:
                    patch[1, 1, 1 + y, slot(1 + index), :] = state.astype(BF16)
                else:
                    spread[pl.ds(y, 128, stride=8), :] = state
            return carry

        lax.fori_loop(0, 4, two_rows, 0)

        def narrow(n, carry):
            rows = pl.ds(pl.multiple_of(n * 256, 256), 256)
            gate_narrow[step, index, rows, :] = gate_wide[rows, :].astype(BF16)
            return carry

        lax.fori_loop(0, 16, narrow, 0)
        stores[step, index].start()
        if step == 1:
            hidden_narrow[index] = spread[...].astype(BF16)
            stores["hidden", index].start()
            stores["memory", index].start()

    stores = {}
    for step in range(2):
        for index in range(2):
            stores[step, index] = pltpu.make_async_copy(
                gate_narrow.at[step, index], gates_out.at[step, index], store_sem.at[step * 2 + index]
            )
    for index in range(2):
        stores["hidden", index] = pltpu.make_async_copy(
            hidden_narrow.at[index], hidden_out.at[index], store_sem.at[4 + index]
        )
        stores["memory", index] = pltpu.make_async_copy(cell.at[index], memory_out.at[index], store_sem.at[6 + index])

    def start(copies):
        for copy in copies:
            copy.start()

    def wait_recv(copies):
        for copy in copies:
            copy.wait_recv()

    loads[0].wait()
    for index in range(2):
        lay_out(hidden_raw[index], 0, 1 + index)
        take_edges(0, 1 + index)
    pl.semaphore_wait(barrier, 17)
    start(messages(0, 2, 2, 2, section))
    start(messages(0, 1, 1, 1, section))

    @pl.when(section == 0)
    def _():
        start(bulk(0))
        start(messages(0, 2, 0, 3, 1))

    loads[1].wait()

    @pl.when(section == 0)
    def _():
        for step in range(2):
            lay_out(frames_raw[step], step, 0)
            take_edges(step, 0)
            start(messages(step, 0, 0, 0, 0))

    loads[2].wait()
    rows = jnp.concatenate([bias_rows[n // 4:n // 4 + 1, (n % 4) * 128:(n % 4 + 1) * 128] for n in range(8)], axis=0)
    columns = jnp.concatenate([rows, jnp.zeros((120, 128), F32)], axis=0).T
    for n in range(8):
        bias[n // 4, (n % 4) * 128:(n % 4 + 1) * 128, :] = jnp.broadcast_to(columns[:, n:n + 1], (128, 128))

    for step in range(2):
        for index in (2, 1):
            wait_recv(messages(step, index, index, index, section))
            insert(step, index)
        if step == 0:
            for n in (3, 4, 5):
                loads[n].wait()
        layer(step, 1)
        if step == 0:
            take_edges(1, 2)

            @pl.when(section == 0)
            def _():
                start(bulk(1))
                start(messages(1, 2, 0, 3, 1))

            start(messages(1, 2, 2, 2, section))

        @pl.when(section == 1)
        def _():
            wait_recv(bulk(step))

        wait_recv(messages(step, 0, 0, 0, 0))
        insert(step, 0)
        layer(step, 0)
        if step == 0:
            take_edges(1, 1)
            start(messages(1, 1, 1, 1, section))

    for step in range(2):
        for index in (1, 2):
            for copy in messages(step, index, index, index, section):
                copy.wait_send()

    @pl.when(section == 0)
    def _():
        for step in range(2):
            for copy in bulk(step) + messages(step, 0, 0, 0, 0) + messages(step, 2, 0, 3, 1):
                copy.wait_send()

    for copy in stores.values():
        copy.wait()


def body(frames, hidden_init, memory_init, weights, biases):
    frames = frames.reshape(2, 1024, 128)
    hidden_init = hidden_init.reshape(2, 1024, 128)
    memory_init = memory_init.reshape(2, 1024, 128)
    vmem = pltpu.VMEM
    dma = pltpu.SemaphoreType.DMA
    hidden_out, memory_out, gates_out = pl.pallas_call(
        kernel,
        out_shape=(
            jax.ShapeDtypeStruct((2, 1024, 128), BF16),
            jax.ShapeDtypeStruct((2, 1024, 128), F32),
            jax.ShapeDtypeStruct((2, 2, 4096, 128), BF16),
        ),
        in_specs=[pl.BlockSpec(memory_space=pl.ANY)] * 5,
        out_specs=[pl.BlockSpec(memory_space=pl.ANY)] * 3,
        scratch_shapes=[
            vmem((2, 3, 10, 384, 128), BF16),
            vmem((1024, 128), F32),
            vmem((2, 1024, 128), BF16),
            vmem((2, 1024, 128), BF16),
            vmem((2, 1024, 128), F32),
            vmem((2, 512, 2304), BF16),
            vmem((2, 512), F32),
            vmem((2, 512, 128), F32),
            vmem((4096, 128), F32),
            vmem((2, 2, 4096, 128), BF16),
            vmem((2, 1024, 128), BF16),
            vmem((2, 3, 2, 16, 128), BF16),
            vmem((2, 3, 6, 16, 128), BF16),
            dma((6,)),
            dma((8,)),
            dma((2, 4, 8)),
            dma((2, 3, 8)),
            dma((2, BULK)),
            dma((2, BULK)),
        ],
        compiler_params=pltpu.CompilerParams(
            collective_id=0, has_side_effects=True, vmem_limit_bytes=56 << 20
        ),
        name="wavefront",
    )(frames, hidden_init, memory_init, weights, biases)
    return (
        hidden_out.reshape(2, 1, 128, 8, 128),
        memory_out.reshape(2, 1, 128, 8, 128),
        gates_out.reshape(2, 2, 1, 512, 8, 128),
    )


def solution(mesh):
    states = P("section", ("member", "tile"), None, None, None)
    in_specs = (
        P(None, ("member", "tile"), None, None, None),
        states,
        states,
        P("section", None, None),
        P("section", None),
    )
    out_specs = (states, states, P(None, "section", ("member", "tile"), None, None, None))
    return jax.shard_map(body, mesh=mesh, in_specs=in_specs, out_specs=out_specs, check_vma=False)
```

time: 124 us -> 71.9 us (0.58)
  the two profiles are of different devices: /device:TPU:128 before, /device:TPU:32 now
where the time goes in v1:
time: 71.9 us; the launch traced here: 71.7 us
  Pallas kernels  62.4 us (87%)
  local copies, waits for them, and re-layouts  8.6 us (12%)
    pallas_call x1, Pallas kernels, body(): pl.pallas_call(kernel, out_shape=(jax.ShapeDtypeStruct((2, 1024, 128), BF...  62.4 us
    unnamed x3, local copies, waits for them, and re-layouts  8.6 us

profile of v1, /device:TPU:32, one launch (start us, length us, event | category | flops | bytes accessed | tf_op | source)
XLA Modules:
  0.0 71.7 jit_solution(5605968120534402678)
XLA Ops:
  0.6 62.4 %wavefront.1 = (bf16[2,1024,128]{2,1,0:T(8,128)(2,1)}, f32[2,1024,128]{2,1,0:T(8,128)}, bf16[2,2,4096,128]{3,2,1,0:T(8,128)(2,1)}) custom-call(bf16[2,1024,128]{2,1,0:T(8,128)(2,1)} %bitcast.15, bf16[2,1024,128]{2,1,0:T(8,128)(2,1)} %bitcast.16, f32[2,1024,128]{2,1,0:T(8,128)} %bitcast.14, bf16[2,512,2304]{2,1,0:T(8,128)(2,1)} %weights.1, f32[2,512]{1,0:T(2,128)} %biases.1), custom_call_target="tpu_custom_call" | custom-call | tf_op jit(solution)/shard_map/wavefront/pallas_call | solution.py:283
  63.0 1.9 %copy.14 = bf16[2,1,128,8,128]{4,3,2,1,0:T(8,128)(2,1)} copy(bf16[2,1,128,8,128]{4,3,2,1,0:T(8,128)(2,1)} %bitcast.17) | data formatting | bytes 1048576
  64.9 2.3 %copy.15 = f32[2,1,128,8,128]{4,3,2,1,0:T(8,128)} copy(f32[2,1,128,8,128]{4,3,2,1,0:T(8,128)} %bitcast.13) | data formatting | bytes 2097152
  67.2 4.5 %copy.16 = bf16[2,2,1,512,8,128]{5,4,3,2,1,0:T(8,128)(2,1)} copy(bf16[2,2,1,512,8,128]{5,4,3,2,1,0:T(8,128)(2,1)} %bitcast.12) | data formatting | bytes 8388608

commit v2 on v1

v2 whole, which is shorter than its diff:
```python
import contextlib

import jax
import jax.numpy as jnp
from jax import lax
from jax.experimental import pallas as pl
from jax.experimental.pallas import tpu as pltpu
from jax.sharding import PartitionSpec as P

GRID_COLS = 8
MESH = pl.DeviceIdType.MESH
F32 = jnp.float32
BF16 = jnp.bfloat16

ROW_UP, ROW_DOWN = 0, 1
NEIGHBOURS = (-8, 8, 1, 9, -7, -1, 7, -9)
UNROLL = 4
CROSS = tuple((row, 1) for row in (1, 8, 2, 3, 4, 5, 6, 7))


def phase(name):
    return contextlib.nullcontext()


def sigmoid(x):
    return 0.5 * jnp.tanh(0.5 * x) + 0.5


def kernel(
    frames, hidden, memory, weights, biases,
    hidden_narrow, cell, gate_narrow,
    patch, spread, hidden_raw, frames_raw, weight, bias_rows, bias,
    gate_wide, partial, edge_send, edge_recv,
    load_sem, send_sem, recv_sem, cross_send, cross_recv,
):
    section = lax.axis_index("section")
    tile = lax.axis_index("tile")
    member = lax.axis_index("member")
    tiles = lax.axis_size("tile")
    place = lax.rem(tile + GRID_COLS + GRID_COLS // 2, tiles)
    grid_row, grid_col = place // GRID_COLS, lax.rem(place, GRID_COLS)
    has_up, has_down = grid_row > 0, grid_row < tiles // GRID_COLS - 1
    has_left, has_right = grid_col > 0, grid_col < GRID_COLS - 1

    def device(which, distance):
        return (which, lax.rem(tile + distance + tiles, tiles), member)

    loads = [
        pltpu.make_async_copy(hidden, hidden_raw, load_sem.at[0]),
        pltpu.make_async_copy(frames, frames_raw, load_sem.at[1]),
        pltpu.make_async_copy(biases, bias_rows, load_sem.at[2]),
        pltpu.make_async_copy(weights.at[1], weight.at[1], load_sem.at[3]),
        pltpu.make_async_copy(memory, cell, load_sem.at[4]),
        pltpu.make_async_copy(weights.at[0], weight.at[0], load_sem.at[5]),
    ]
    for load in loads:
        load.start()

    barrier = pltpu.get_barrier_semaphore()
    for distance in NEIGHBOURS:
        pl.semaphore_signal(barrier, 1, device_id=device(section, distance), device_id_type=MESH)
    pl.semaphore_signal(barrier, 1, device_id=device(1 - section, 0), device_id_type=MESH)

    def slot(index):
        return pl.ds(index * 128, 128)

    def message(step, source, target, flow, which, number):
        if number == ROW_UP:
            src = patch.at[step, 1, 1, slot(source)]
            dst = patch.at[step, 1, 9, slot(target)]
        elif number == ROW_DOWN:
            src = patch.at[step, 1, 8, slot(source)]
            dst = patch.at[step, 1, 0, slot(target)]
        else:
            src = edge_send.at[step, source, 0 if number < 5 else 1]
            dst = edge_recv.at[step, target, number - 2]
        return pltpu.make_async_remote_copy(
            src_ref=src, dst_ref=dst,
            send_sem=send_sem.at[step, flow, number], recv_sem=recv_sem.at[step, target, number],
            device_id=device(which, NEIGHBOURS[number]), device_id_type=MESH,
        )

    def messages(step, source, target, flow, which):
        return [message(step, source, target, flow, which, n) for n in range(8)]

    def cross(step):
        copies = [(edge_send.at[step, 2], edge_send.at[step, 0])]
        for first, count in CROSS:
            rows = pl.ds(first, count)
            copies.append((patch.at[step, 1, rows, slot(2)], patch.at[step, 1, rows, slot(0)]))
        return [
            pltpu.make_async_remote_copy(
                src_ref=src, dst_ref=dst, send_sem=cross_send.at[step, n], recv_sem=cross_recv.at[step, n],
                device_id=device(1, 0), device_id_type=MESH,
            )
            for n, (src, dst) in enumerate(copies)
        ]

    def lay_out(raw, step, index):
        spread[...] = raw.astype(F32)
        for y in range(8):
            patch[step, 1, 1 + y, slot(index), :] = spread[pl.ds(y, 128, stride=8), :].astype(BF16)

    row_of = lax.broadcasted_iota(jnp.int32, (16, 128), 0)
    lane_of = lax.broadcasted_iota(jnp.int32, (16, 128), 1)

    def take_edges(step, index):
        left = jnp.zeros((16, 128), F32)
        right = jnp.zeros((16, 128), F32)
        for y in range(8):
            pick = jnp.concatenate(
                [((row_of == y) & (lane_of == 0)).astype(F32), ((row_of == y) & (lane_of == 127)).astype(F32)], axis=0
            ).astype(BF16)
            both = lax.dot_general(
                pick, patch[step, 1, 1 + y, slot(index), :], (((1,), (1,)), ((), ())), preferred_element_type=F32
            )
            left += both[:16]
            right += both[16:]
        edge_send[step, index, 0] = right.astype(BF16)
        edge_send[step, index, 1] = left.astype(BF16)

    lane = lax.broadcasted_iota(jnp.int32, (128, 128), 1)

    def insert(step, index):
        edges = edge_recv[step, index].reshape(96, 128).astype(F32)
        edges = jnp.concatenate([edges, jnp.zeros((32, 128), F32)], axis=0).T

        def one_row(r, left_at, right_at, live):
            x = patch[step, 1, r, slot(index), :].astype(F32)
            if live is not None:
                x = jnp.where(live, x, 0.0)
                patch[step, 1, r, slot(index), :] = x.astype(BF16)
            from_left = jnp.where(has_left if live is None else live & has_left, pltpu.roll(edges, 128 - left_at, 1), 0.0)
            from_right = jnp.where(has_right if live is None else live & has_right, pltpu.roll(edges, 127 - right_at, 1), 0.0)
            patch[step, 0, r, slot(index), :] = jnp.where(lane == 0, from_left, pltpu.roll(x, 1, 1)).astype(BF16)
            patch[step, 2, r, slot(index), :] = jnp.where(lane == 127, from_right, pltpu.roll(x, 127, 1)).astype(BF16)

        def inner_row(r, carry):
            one_row(r, r - 1, r + 47, None)
            return carry

        one_row(0, 23, 71, has_up)
        one_row(9, 32, 80, has_down)
        lax.fori_loop(1, 9, inner_row, 0, unroll=4)

    def product(step, index, pair, parts):
        chunks = [(tap, part) for tap in range(9) for part in parts]
        acc = None
        for first in range(0, len(chunks), 2):
            group = chunks[first:first + 2]
            lhs = jnp.concatenate(
                [weight[index, :, tap * 256 + part * 128:tap * 256 + part * 128 + 128] for tap, part in group], axis=1
            )
            rhs = jnp.concatenate(
                [
                    jnp.concatenate(
                        [patch[step, tap % 3, 2 * pair + r + tap // 3, slot(index + part), :] for r in range(2)], axis=1
                    )
                    for tap, part in group
                ],
                axis=0,
            )
            dot = jnp.dot(lhs, rhs, preferred_element_type=F32)
            acc = dot if acc is None else acc + dot
        return acc

    def first_half(step, index):
        def two_rows(pair, carry):
            offset = jnp.concatenate([bias[index]] * 2, axis=1)
            partial[pair] = product(step, index, pair, (1,)) + offset
            return carry

        lax.fori_loop(0, 4, two_rows, 0, unroll=UNROLL)

    def layer(step, index, whole):
        def two_rows(pair, carry):
            if whole:
                acc = product(step, index, pair, (0, 1)) + jnp.concatenate([bias[index]] * 2, axis=1)
            else:
                acc = product(step, index, pair, (0,)) + partial[pair]
            for r in range(2):
                y = 2 * pair + r
                pre = acc[:, r * 128:(r + 1) * 128]
                inflow = sigmoid(pre[0:128])
                forget = sigmoid(pre[128:256])
                outflow = sigmoid(pre[256:384])
                candidate = jnp.tanh(pre[384:512])
                for n, gate in enumerate((inflow, forget, outflow, candidate)):
                    gate_wide[pl.ds(y + n * 1024, 128, stride=8), :] = gate
                old = cell[index, pl.ds(y, 128, stride=8), :]
                new = forget * old + inflow * candidate
                cell[index, pl.ds(y, 128, stride=8), :] = new
                state = outflow * jnp.tanh(new)
                if step == 0:
                    patch[1, 1, 1 + y, slot(1 + index), :] = state.astype(BF16)
                else:
                    spread[pl.ds(y, 128, stride=8), :] = state
            return carry

        lax.fori_loop(0, 4, two_rows, 0, unroll=UNROLL)

    def finish(step, index):
        def narrow(n, carry):
            rows = pl.ds(pl.multiple_of(n * 256, 256), 256)
            gate_narrow[step, index, rows, :] = gate_wide[rows, :].astype(BF16)
            return carry

        lax.fori_loop(0, 16, narrow, 0, unroll=4)
        if step == 1:
            hidden_narrow[index] = spread[...].astype(BF16)

    def start(copies):
        for copy in copies:
            copy.start()

    def wait_recv(copies):
        for copy in copies:
            copy.wait_recv()

    def wait_send(copies):
        for copy in copies:
            copy.wait_send()

    def on(which, action):
        pl.when(section == which)(action)

    with phase("load"):
        loads[0].wait()
    with phase("lay"):
        for index in range(2):
            lay_out(hidden_raw[index], 0, 1 + index)
            take_edges(0, 1 + index)
    with phase("framesprep"):
        loads[1].wait()

        @pl.when(section == 0)
        def _():
            for step in range(2):
                lay_out(frames_raw[step], step, 0)
                take_edges(step, 0)

    with phase("barrier"):
        pl.semaphore_wait(barrier, 9)
    with phase("send0"):
        start(messages(0, 2, 2, 2, section))
        start(messages(0, 1, 1, 1, section))

        @pl.when(section == 0)
        def _():
            start(messages(0, 0, 0, 0, section))
            start(cross(0))

    with phase("bias"):
        loads[2].wait()
        rows = jnp.concatenate([bias_rows[n // 4:n // 4 + 1, (n % 4) * 128:(n % 4 + 1) * 128] for n in range(8)], axis=0)
        columns = jnp.concatenate([rows, jnp.zeros((120, 128), F32)], axis=0).T
        for n in range(8):
            bias[n // 4, (n % 4) * 128:(n % 4 + 1) * 128, :] = jnp.broadcast_to(columns[:, n:n + 1], (128, 128))

    depth = tile // 16
    inner = (depth == 1) | (depth == 2)

    def take_in(step, index, first=0):
        with phase(f"wait_halo_s{step}_{index}"):
            wait_recv(messages(step, index, index, index, section)[first:])
        with phase(f"insert_s{step}_{index}"):
            insert(step, index)

    def pass_on(step):
        with phase(f"pass_on_s{step}"):
            @pl.when(section == 1)
            def _():
                wait_recv(cross(step)[:3])
                start(messages(step, 0, 0, 0, section))

    def rest(step):
        with phase(f"wait_rest_s{step}"):
            @pl.when(section == 1)
            def _():
                wait_recv(cross(step)[3:])

    take_in(0, 2)
    take_in(0, 1)
    with phase("wait_w"):
        for n in (3, 4, 5):
            loads[n].wait()
    with phase("layer_s0_1"):
        layer(0, 1, True)
    with phase("send1"):
        start(messages(1, 2, 2, 2, section)[:2])
        take_edges(1, 2)
        start(messages(1, 2, 2, 2, section)[2:])

        @pl.when((section == 0) & inner)
        def _():
            start(cross(1))

        @pl.when(section == 0)
        def _():
            start(messages(1, 0, 0, 0, section))

    pass_on(0)
    with phase("finish_s0_1"):
        finish(0, 1)
    with phase("half_s0_0"):
        first_half(0, 0)
    rest(0)
    take_in(0, 0)
    with phase("layer_s0_0"):
        layer(0, 0, False)
    with phase("send2"):
        start(messages(1, 1, 1, 1, section)[:2])
        take_edges(1, 1)
        start(messages(1, 1, 1, 1, section)[2:])

    with phase("finish_s0_0"):
        finish(0, 0)
    take_in(1, 2)
    with phase("half_s1_1"):
        first_half(1, 1)

    @pl.when((section == 0) & jnp.logical_not(inner))
    def _():
        start(cross(1))

    pass_on(1)
    take_in(1, 1)
    with phase("layer_s1_1"):
        layer(1, 1, False)
    with phase("finish_s1_1"):
        finish(1, 1)
    with phase("half_s1_0"):
        first_half(1, 0)
    rest(1)
    take_in(1, 0)
    with phase("layer_s1_0"):
        layer(1, 0, False)
    with phase("finish_s1_0"):
        finish(1, 0)

    for step in range(2):
        for index in range(3):
            wait_send(messages(step, index, index, index, section))

    @pl.when(section == 0)
    def _():
        for step in range(2):
            wait_send(cross(step))


def write_out(*refs):
    sources, targets, sem = refs[:3], refs[3:6], refs[6]
    copies = [pltpu.make_async_copy(src, dst, sem.at[n]) for n, (src, dst) in enumerate(zip(sources, targets))]
    for copy in copies:
        copy.start()
    for copy in copies:
        copy.wait()


def body(frames, hidden_init, memory_init, weights, biases):
    frames = frames.reshape(2, 1024, 128)
    hidden_init = hidden_init.reshape(2, 1024, 128)
    memory_init = memory_init.reshape(2, 1024, 128)
    vmem = pltpu.VMEM
    dma = pltpu.SemaphoreType.DMA
    shapes = (
        jax.ShapeDtypeStruct((2, 1024, 128), BF16),
        jax.ShapeDtypeStruct((2, 1024, 128), F32),
        jax.ShapeDtypeStruct((2, 2, 4096, 128), BF16),
    )
    results = pl.pallas_call(
        kernel,
        out_shape=shapes,
        in_specs=[pl.BlockSpec(memory_space=pltpu.HBM)] * 5,
        out_specs=[pl.BlockSpec(memory_space=pltpu.VMEM)] * 3,
        scratch_shapes=[
            vmem((2, 3, 10, 384, 128), BF16),
            vmem((1024, 128), F32),
            vmem((2, 1024, 128), BF16),
            vmem((2, 1024, 128), BF16),
            vmem((2, 512, 2304), BF16),
            vmem((2, 512), F32),
            vmem((2, 512, 128), F32),
            vmem((4096, 128), F32),
            vmem((4, 512, 256), F32),
            vmem((2, 3, 2, 16, 128), BF16),
            vmem((2, 3, 6, 16, 128), BF16),
            dma((6,)),
            dma((2, 3, 8)),
            dma((2, 3, 8)),
            dma((2, 1 + len(CROSS))),
            dma((2, 1 + len(CROSS))),
        ],
        compiler_params=pltpu.CompilerParams(
            collective_id=0, has_side_effects=True, vmem_limit_bytes=32 << 20
        ),
        name="wavefront",
    )(*[pltpu.with_memory_space_constraint(x, pltpu.HBM) for x in (frames, hidden_init, memory_init, weights, biases)])
    hidden_out, memory_out, gates_out = pl.pallas_call(
        write_out,
        out_shape=shapes,
        in_specs=[pl.BlockSpec(memory_space=pl.ANY)] * 3,
        out_specs=[pl.BlockSpec(memory_space=pltpu.HBM)] * 3,
        scratch_shapes=[dma((3,))],
        compiler_params=pltpu.CompilerParams(vmem_limit_bytes=1 << 20),
        name="write_out",
    )(*results)
    return (
        hidden_out.reshape(2, 1, 128, 8, 128),
        memory_out.reshape(2, 1, 128, 8, 128),
        gates_out.reshape(2, 2, 1, 512, 8, 128),
    )


def solution(mesh):
    states = P("section", ("member", "tile"), None, None, None)
    in_specs = (
        P(None, ("member", "tile"), None, None, None),
        states,
        states,
        P("section", None, None),
        P("section", None),
    )
    out_specs = (states, states, P(None, "section", ("member", "tile"), None, None, None))
    return jax.shard_map(body, mesh=mesh, in_specs=in_specs, out_specs=out_specs, check_vma=False)
```

time: 71.9 us -> 52.9 us (0.74)
  the two profiles are of different devices: /device:TPU:32 before, /device:TPU:128 now
where the time goes in v2:
time: 52.9 us; the launch traced here: 52.8 us
  Pallas kernels  52.2 us (99%)
  between operations  0.64 us (1%)
    pallas_call x1, Pallas kernels, body(): pl.pallas_call(kernel, out_shape=shapes, in_specs=[pl.BlockSpec(memory_sp...  49.6 us
    pallas_call x1, Pallas kernels, body(): pl.pallas_call(write_out, out_shape=shapes, in_specs=[pl.BlockSpec(memory...  2.56 us

profile of v2, /device:TPU:128, one launch (start us, length us, event | category | flops | bytes accessed | tf_op | source)
XLA Modules:
  0.0 52.8 jit_solution(15549911009000451844)
XLA Ops:
  0.6 49.6 %wavefront.1 = (bf16[2,1024,128]{2,1,0:T(8,128)(2,1)S(1)}, f32[2,1024,128]{2,1,0:T(8,128)S(1)}, bf16[2,2,4096,128]{3,2,1,0:T(8,128)(2,1)S(1)}) custom-call(bf16[2,1024,128]{2,1,0:T(8,128)(2,1)} %bitcast.13, bf16[2,1024,128]{2,1,0:T(8,128)(2,1)} %bitcast.14, f32[2,1024,128]{2,1,0:T(8,128)} %bitcast.12, bf16[2,512,2304]{2,1,0:T(8,128)(2,1)} %weights.1, ...), custom_call_target="tpu_custom_call" | custom-call | tf_op jit(solution)/shard_map/wavefront/pallas_call | solution.py:371
  50.3 2.6 %write_out.1 = (bf16[2,1024,128]{2,1,0:T(8,128)(2,1)}, f32[2,1024,128]{2,1,0:T(8,128)}, bf16[2,2,4096,128]{3,2,1,0:T(8,128)(2,1)}) custom-call(bf16[2,1024,128]{2,1,0:T(8,128)(2,1)S(1)} %get-tuple-element.9.refs_0_, f32[2,1024,128]{2,1,0:T(8,128)S(1)} %get-tuple-element.10.refs_1_, bf16[2,2,4096,128]{3,2,1,0:T(8,128)(2,1)S(1)} %get-tuple-element.11.refs_2_), custom_call_target="tpu_custom_call" | custom-call | tf_op jit(solution)/shard_map/write_out/pallas_call | solution.py:399

commit v3 on v2

--- a/solution.py
+++ b/solution.py
@@ -14,7 +14,6 @@
 
 ROW_UP, ROW_DOWN = 0, 1
 NEIGHBOURS = (-8, 8, 1, 9, -7, -1, 7, -9)
-UNROLL = 4
 CROSS = tuple((row, 1) for row in (1, 8, 2, 3, 4, 5, 6, 7))
 
 
@@ -31,7 +30,7 @@
     hidden_narrow, cell, gate_narrow,
     patch, spread, hidden_raw, frames_raw, weight, bias_rows, bias,
     gate_wide, partial, edge_send, edge_recv,
-    load_sem, send_sem, recv_sem, cross_send, cross_recv,
+    load_sem, send_sem, recv_sem, cross_send, cross_recv, turn,
 ):
     section = lax.axis_index("section")
     tile = lax.axis_index("tile")
@@ -59,7 +58,10 @@
     barrier = pltpu.get_barrier_semaphore()
     for distance in NEIGHBOURS:
         pl.semaphore_signal(barrier, 1, device_id=device(section, distance), device_id_type=MESH)
+    depth = tile // 16
+    beside = device(section, jnp.where(lax.rem(depth, 2) == 0, 16, -16))
     pl.semaphore_signal(barrier, 1, device_id=device(1 - section, 0), device_id_type=MESH)
+    pl.semaphore_signal(barrier, 1, device_id=beside, device_id_type=MESH)
 
     def slot(index):
         return pl.ds(index * 128, 128)
@@ -101,12 +103,12 @@
         for y in range(8):
             patch[step, 1, 1 + y, slot(index), :] = spread[pl.ds(y, 128, stride=8), :].astype(BF16)
 
-    row_of = lax.broadcasted_iota(jnp.int32, (16, 128), 0)
-    lane_of = lax.broadcasted_iota(jnp.int32, (16, 128), 1)
+    row_of = lax.broadcasted_iota(jnp.int32, (8, 128), 0)
+    lane_of = lax.broadcasted_iota(jnp.int32, (8, 128), 1)
 
     def take_edges(step, index):
-        left = jnp.zeros((16, 128), F32)
-        right = jnp.zeros((16, 128), F32)
+        left = jnp.zeros((8, 128), F32)
+        right = jnp.zeros((8, 128), F32)
         for y in range(8):
             pick = jnp.concatenate(
                 [((row_of == y) & (lane_of == 0)).astype(F32), ((row_of == y) & (lane_of == 127)).astype(F32)], axis=0
@@ -114,34 +116,40 @@
             both = lax.dot_general(
                 pick, patch[step, 1, 1 + y, slot(index), :], (((1,), (1,)), ((), ())), preferred_element_type=F32
             )
-            left += both[:16]
-            right += both[16:]
+            left += both[:8]
+            right += both[8:]
         edge_send[step, index, 0] = right.astype(BF16)
         edge_send[step, index, 1] = left.astype(BF16)
 
     lane = lax.broadcasted_iota(jnp.int32, (128, 128), 1)
 
+    def put(step, b, r, index, value):
+        patch[step, b, r, slot(index), :] = value.astype(BF16)
+
+    def shift(step, index):
+        for r in range(1, 9):
+            x = patch[step, 1, r, slot(index), :].astype(F32)
+            put(step, 0, r, index, pltpu.roll(x, 1, 1))
+            put(step, 2, r, index, pltpu.roll(x, 127, 1))
+
     def insert(step, index):
-        edges = edge_recv[step, index].reshape(96, 128).astype(F32)
-        edges = jnp.concatenate([edges, jnp.zeros((32, 128), F32)], axis=0).T
-
-        def one_row(r, left_at, right_at, live):
-            x = patch[step, 1, r, slot(index), :].astype(F32)
-            if live is not None:
-                x = jnp.where(live, x, 0.0)
-                patch[step, 1, r, slot(index), :] = x.astype(BF16)
-            from_left = jnp.where(has_left if live is None else live & has_left, pltpu.roll(edges, 128 - left_at, 1), 0.0)
-            from_right = jnp.where(has_right if live is None else live & has_right, pltpu.roll(edges, 127 - right_at, 1), 0.0)
-            patch[step, 0, r, slot(index), :] = jnp.where(lane == 0, from_left, pltpu.roll(x, 1, 1)).astype(BF16)
-            patch[step, 2, r, slot(index), :] = jnp.where(lane == 127, from_right, pltpu.roll(x, 127, 1)).astype(BF16)
-
-        def inner_row(r, carry):
-            one_row(r, r - 1, r + 47, None)
-            return carry
-
-        one_row(0, 23, 71, has_up)
-        one_row(9, 32, 80, has_down)
-        lax.fori_loop(1, 9, inner_row, 0, unroll=4)
+        edges = edge_recv[step, index].astype(F32).reshape(48, 128)
+        edges = jnp.concatenate([edges, jnp.zeros((80, 128), F32)], axis=0).T
+        for r, left_at, right_at in [(0, 15, 39), (9, 16, 40)] + [(r, r - 1, r + 23) for r in range(1, 9)]:
+            live_left, live_right = has_left, has_right
+            if r in (0, 9):
+                live = has_up if r == 0 else has_down
+                live_left, live_right = live & has_left, live & has_right
+                x = jnp.where(live, patch[step, 1, r, slot(index), :].astype(F32), 0.0)
+                put(step, 1, r, index, x)
+                to_right, to_left = pltpu.roll(x, 1, 1), pltpu.roll(x, 127, 1)
+            else:
+                to_right = patch[step, 0, r, slot(index), :].astype(F32)
+                to_left = patch[step, 2, r, slot(index), :].astype(F32)
+            from_left = jnp.where(live_left, pltpu.roll(edges, (128 - left_at) % 128, 1), 0.0)
+            from_right = jnp.where(live_right, pltpu.roll(edges, 127 - right_at, 1), 0.0)
+            put(step, 0, r, index, jnp.where(lane == 0, from_left, to_right))
+            put(step, 2, r, index, jnp.where(lane == 127, from_right, to_left))
 
     def product(step, index, pair, parts):
         chunks = [(tap, part) for tap in range(9) for part in parts]
@@ -164,20 +172,18 @@
             acc = dot if acc is None else acc + dot
         return acc
 
-    def first_half(step, index):
-        def two_rows(pair, carry):
+    def first_half(step, index, part):
+        for pair in range(4):
             offset = jnp.concatenate([bias[index]] * 2, axis=1)
-            partial[pair] = product(step, index, pair, (1,)) + offset
-            return carry
-
-        lax.fori_loop(0, 4, two_rows, 0, unroll=UNROLL)
-
-    def layer(step, index, whole):
-        def two_rows(pair, carry):
-            if whole:
-                acc = product(step, index, pair, (0, 1)) + jnp.concatenate([bias[index]] * 2, axis=1)
+            partial[index, pair] = product(step, index, pair, (part,)) + offset
+
+    def layer(step, index, parts, pairs=(0, 3, 1, 2)):
+        for pair in pairs:
+            acc = product(step, index, pair, parts)
+            if len(parts) == 2:
+                acc += jnp.concatenate([bias[index]] * 2, axis=1)
             else:
-                acc = product(step, index, pair, (0,)) + partial[pair]
+                acc += partial[index, pair]
             for r in range(2):
                 y = 2 * pair + r
                 pre = acc[:, r * 128:(r + 1) * 128]
@@ -195,9 +201,6 @@
                     patch[1, 1, 1 + y, slot(1 + index), :] = state.astype(BF16)
                 else:
                     spread[pl.ds(y, 128, stride=8), :] = state
-            return carry
-
-        lax.fori_loop(0, 4, two_rows, 0, unroll=UNROLL)
 
     def finish(step, index):
         def narrow(n, carry):
@@ -223,6 +226,26 @@
 
     def on(which, action):
         pl.when(section == which)(action)
+
+    between = (depth == 1) | (depth == 2)
+    inner, outer = (section == 0) & between, (section == 0) & jnp.logical_not(between)
+
+    def hand_over(step, who):
+        @pl.when(who)
+        def _():
+            start(cross(step))
+
+    def pass_turn(who, copies):
+        @pl.when(who)
+        def _():
+            wait_send(copies)
+            pl.semaphore_signal(turn, 1, device_id=beside, device_id_type=MESH)
+
+    def take_turn(who, copies):
+        @pl.when(who)
+        def _():
+            pl.semaphore_wait(turn, 1)
+            start(copies)
 
     with phase("load"):
         loads[0].wait()
@@ -238,9 +261,10 @@
             for step in range(2):
                 lay_out(frames_raw[step], step, 0)
                 take_edges(step, 0)
+                shift(step, 0)
 
     with phase("barrier"):
-        pl.semaphore_wait(barrier, 9)
+        pl.semaphore_wait(barrier, 10)
     with phase("send0"):
         start(messages(0, 2, 2, 2, section))
         start(messages(0, 1, 1, 1, section))
@@ -248,8 +272,12 @@
         @pl.when(section == 0)
         def _():
             start(messages(0, 0, 0, 0, section))
-            start(cross(0))
-
+
+        hand_over(0, outer)
+
+    with phase("shift0"):
+        shift(0, 2)
+        shift(0, 1)
     with phase("bias"):
         loads[2].wait()
         rows = jnp.concatenate([bias_rows[n // 4:n // 4 + 1, (n % 4) * 128:(n % 4 + 1) * 128] for n in range(8)], axis=0)
@@ -257,18 +285,15 @@
         for n in range(8):
             bias[n // 4, (n % 4) * 128:(n % 4 + 1) * 128, :] = jnp.broadcast_to(columns[:, n:n + 1], (128, 128))
 
-    depth = tile // 16
-    inner = (depth == 1) | (depth == 2)
-
     def take_in(step, index, first=0):
         with phase(f"wait_halo_s{step}_{index}"):
             wait_recv(messages(step, index, index, index, section)[first:])
         with phase(f"insert_s{step}_{index}"):
             insert(step, index)
 
-    def pass_on(step):
+    def pass_on(step, who):
         with phase(f"pass_on_s{step}"):
-            @pl.when(section == 1)
+            @pl.when((section == 1) & who)
             def _():
                 wait_recv(cross(step)[:3])
                 start(messages(step, 0, 0, 0, section))
@@ -278,63 +303,68 @@
             @pl.when(section == 1)
             def _():
                 wait_recv(cross(step)[3:])
+                shift(step, 0)
 
     take_in(0, 2)
     take_in(0, 1)
+    with phase("turn0"):
+        pass_turn(outer, cross(0))
+        take_turn(inner, cross(0))
     with phase("wait_w"):
         for n in (3, 4, 5):
             loads[n].wait()
     with phase("layer_s0_1"):
-        layer(0, 1, True)
+        layer(0, 1, (0, 1), (0, 3))
+        start(messages(1, 2, 2, 2, section)[:2])
+        layer(0, 1, (0, 1), (1, 2))
     with phase("send1"):
-        start(messages(1, 2, 2, 2, section)[:2])
         take_edges(1, 2)
         start(messages(1, 2, 2, 2, section)[2:])
 
-        @pl.when((section == 0) & inner)
-        def _():
-            start(cross(1))
-
         @pl.when(section == 0)
         def _():
             start(messages(1, 0, 0, 0, section))
 
-    pass_on(0)
+    pass_on(0, jnp.logical_not(between))
     with phase("finish_s0_1"):
         finish(0, 1)
+        shift(1, 2)
     with phase("half_s0_0"):
-        first_half(0, 0)
+        first_half(0, 0, 1)
+    pass_on(0, between)
     rest(0)
     take_in(0, 0)
     with phase("layer_s0_0"):
-        layer(0, 0, False)
+        layer(0, 0, (0,), (0, 3))
+        start(messages(1, 1, 1, 1, section)[:2])
+        layer(0, 0, (0,), (1, 2))
     with phase("send2"):
-        start(messages(1, 1, 1, 1, section)[:2])
         take_edges(1, 1)
         start(messages(1, 1, 1, 1, section)[2:])
+        hand_over(1, inner)
 
     with phase("finish_s0_0"):
         finish(0, 0)
+        shift(1, 1)
+    pass_on(1, between)
     take_in(1, 2)
     with phase("half_s1_1"):
-        first_half(1, 1)
-
-    @pl.when((section == 0) & jnp.logical_not(inner))
-    def _():
-        start(cross(1))
-
-    pass_on(1)
+        first_half(1, 1, 1)
+    with phase("turn1"):
+        pass_turn(inner, cross(0) + cross(1))
+        take_turn(outer, cross(1))
+    pass_on(1, jnp.logical_not(between))
     take_in(1, 1)
     with phase("layer_s1_1"):
-        layer(1, 1, False)
+        layer(1, 1, (0,))
+    with phase("half_s1_0"):
+        first_half(1, 0, 1)
     with phase("finish_s1_1"):
         finish(1, 1)
-    with phase("half_s1_0"):
-        first_half(1, 0)
     rest(1)
     take_in(1, 0)
     with phase("layer_s1_0"):
-        layer(1, 0, False)
+        layer(1, 0, (0,))
     with phase("finish_s1_0"):
         finish(1, 0)
 
@@ -342,10 +372,9 @@
         for index in range(3):
             wait_send(messages(step, index, index, index, section))
 
-    @pl.when(section == 0)
+    @pl.when(outer)
     def _():
-        for step in range(2):
-            wait_send(cross(step))
+        wait_send(cross(1))
 
 
 def write_out(*refs):
@@ -382,14 +411,15 @@
             vmem((2, 512), F32),
             vmem((2, 512, 128), F32),
             vmem((4096, 128), F32),
-            vmem((4, 512, 256), F32),
-            vmem((2, 3, 2, 16, 128), BF16),
-            vmem((2, 3, 6, 16, 128), BF16),
+            vmem((2, 4, 512, 256), F32),
+            vmem((2, 3, 2, 8, 128), BF16),
+            vmem((2, 3, 6, 8, 128), BF16),
             dma((6,)),
             dma((2, 3, 8)),
             dma((2, 3, 8)),
             dma((2, 1 + len(CROSS))),
             dma((2, 1 + len(CROSS))),
+            pltpu.SemaphoreType.REGULAR,
         ],
         compiler_params=pltpu.CompilerParams(
             collective_id=0, has_side_effects=True, vmem_limit_bytes=32 << 20

time: 52.9 us -> 48.5 us (0.917)
  Pallas kernels: 52.2 us -> 47.8 us
    pallas_call x1, Pallas kernels: 49.6 us -> 45.2 us  [body(): pl.pallas_call(kernel, out_shape=shapes, in_specs=[pl.BlockSpec(memory_sp...]
where the time goes in v3:
time: 48.5 us; the launch traced here: 48.4 us
  Pallas kernels  47.8 us (99%)
  between operations  0.64 us (1%)
    pallas_call x1, Pallas kernels, body(): pl.pallas_call(kernel, out_shape=shapes, in_specs=[pl.BlockSpec(memory_sp...  45.2 us
    pallas_call x1, Pallas kernels, body(): pl.pallas_call(write_out, out_shape=shapes, in_specs=[pl.BlockSpec(memory...  2.56 us

profile of v3, /device:TPU:128, one launch (start us, length us, event | category | flops | bytes accessed | tf_op | source)
XLA Modules:
  0.0 48.4 jit_solution(11434073229412790567)
XLA Ops:
  0.6 45.2 %wavefront.1 = (bf16[2,1024,128]{2,1,0:T(8,128)(2,1)S(1)}, f32[2,1024,128]{2,1,0:T(8,128)S(1)}, bf16[2,2,4096,128]{3,2,1,0:T(8,128)(2,1)S(1)}) custom-call(bf16[2,1024,128]{2,1,0:T(8,128)(2,1)} %bitcast.13, bf16[2,1024,128]{2,1,0:T(8,128)(2,1)} %bitcast.14, f32[2,1024,128]{2,1,0:T(8,128)} %bitcast.12, bf16[2,512,2304]{2,1,0:T(8,128)(2,1)} %weights.1, ...), custom_call_target="tpu_custom_call" | custom-call | tf_op jit(solution)/shard_map/wavefront/pallas_call | solution.py:400
  45.8 2.6 %write_out.1 = (bf16[2,1024,128]{2,1,0:T(8,128)(2,1)}, f32[2,1024,128]{2,1,0:T(8,128)}, bf16[2,2,4096,128]{3,2,1,0:T(8,128)(2,1)}) custom-call(bf16[2,1024,128]{2,1,0:T(8,128)(2,1)S(1)} %get-tuple-element.9.refs_0_, f32[2,1024,128]{2,1,0:T(8,128)S(1)} %get-tuple-element.10.refs_1_, bf16[2,2,4096,128]{3,2,1,0:T(8,128)(2,1)S(1)} %get-tuple-element.11.refs_2_), custom_call_target="tpu_custom_call" | custom-call | tf_op jit(solution)/shard_map/write_out/pallas_call | solution.py:429

commit v4 on v3

--- a/solution.py
+++ b/solution.py
@@ -25,13 +25,45 @@
     return 0.5 * jnp.tanh(0.5 * x) + 0.5
 
 
+def products(weight, rows_of, pair, parts):
+    chunks = [(tap, part) for tap in range(9) for part in parts]
+    acc = None
+    for first in range(0, len(chunks), 2):
+        group = chunks[first:first + 2]
+        lhs = jnp.concatenate(
+            [weight[:, tap * 256 + part * 128:tap * 256 + part * 128 + 128] for tap, part in group], axis=1
+        )
+        rhs = jnp.concatenate(
+            [jnp.concatenate([rows_of(tap, part, 2 * pair + r) for r in range(2)], axis=1) for tap, part in group],
+            axis=0,
+        )
+        dot = jnp.dot(lhs, rhs, preferred_element_type=F32)
+        acc = dot if acc is None else acc + dot
+    return acc
+
+
+def advance(pre, old):
+    inflow = sigmoid(pre[0:128])
+    forget = sigmoid(pre[128:256])
+    outflow = sigmoid(pre[256:384])
+    candidate = jnp.tanh(pre[384:512])
+    new = forget * old + inflow * candidate
+    return (inflow, forget, outflow, candidate), new, outflow * jnp.tanh(new)
+
+
+def spread_gates(gate_wide, y, gates):
+    for n, gate in enumerate(gates):
+        gate_wide[pl.ds(y + n * 1024, 128, stride=8), :] = gate
+
+
 def kernel(
     frames, hidden, memory, weights, biases,
-    hidden_narrow, cell, gate_narrow,
-    patch, spread, hidden_raw, frames_raw, weight, bias_rows, bias,
-    gate_wide, partial, edge_send, edge_recv,
+    gate_narrow, hidden_narrow, cell, window, partial_first, weight_first,
+    patch, spread, hidden_raw, frames_raw, weight_second, bias_rows, bias,
+    gate_wide, partial_second, edge_send, edge_recv,
     load_sem, send_sem, recv_sem, cross_send, cross_recv, turn,
 ):
+    weight, partial = (weight_first, weight_second), (partial_first, partial_second)
     section = lax.axis_index("section")
     tile = lax.axis_index("tile")
     member = lax.axis_index("member")
@@ -48,9 +80,9 @@
         pltpu.make_async_copy(hidden, hidden_raw, load_sem.at[0]),
         pltpu.make_async_copy(frames, frames_raw, load_sem.at[1]),
         pltpu.make_async_copy(biases, bias_rows, load_sem.at[2]),
-        pltpu.make_async_copy(weights.at[1], weight.at[1], load_sem.at[3]),
+        pltpu.make_async_copy(weights.at[1], weight[1], load_sem.at[3]),
         pltpu.make_async_copy(memory, cell, load_sem.at[4]),
-        pltpu.make_async_copy(weights.at[0], weight.at[0], load_sem.at[5]),
+        pltpu.make_async_copy(weights.at[0], weight[0], load_sem.at[5]),
     ]
     for load in loads:
         load.start()
@@ -152,30 +184,14 @@
             put(step, 2, r, index, jnp.where(lane == 127, from_right, to_left))
 
     def product(step, index, pair, parts):
-        chunks = [(tap, part) for tap in range(9) for part in parts]
-        acc = None
-        for first in range(0, len(chunks), 2):
-            group = chunks[first:first + 2]
-            lhs = jnp.concatenate(
-                [weight[index, :, tap * 256 + part * 128:tap * 256 + part * 128 + 128] for tap, part in group], axis=1
-            )
-            rhs = jnp.concatenate(
-                [
-                    jnp.concatenate(
-                        [patch[step, tap % 3, 2 * pair + r + tap // 3, slot(index + part), :] for r in range(2)], axis=1
-                    )
-                    for tap, part in group
-                ],
-                axis=0,
-            )
-            dot = jnp.dot(lhs, rhs, preferred_element_type=F32)
-            acc = dot if acc is None else acc + dot
-        return acc
+        return products(
+            weight[index], lambda tap, part, y: patch[step, tap % 3, y + tap // 3, slot(index + part), :], pair, parts
+        )
 
     def first_half(step, index, part):
         for pair in range(4):
             offset = jnp.concatenate([bias[index]] * 2, axis=1)
-            partial[index, pair] = product(step, index, pair, (part,)) + offset
+            partial[index][pair] = product(step, index, pair, (part,)) + offset
 
     def layer(step, index, parts, pairs=(0, 3, 1, 2)):
         for pair in pairs:
@@ -183,20 +199,13 @@
             if len(parts) == 2:
                 acc += jnp.concatenate([bias[index]] * 2, axis=1)
             else:
-                acc += partial[index, pair]
+                acc += partial[index][pair]
             for r in range(2):
                 y = 2 * pair + r
-                pre = acc[:, r * 128:(r + 1) * 128]
-                inflow = sigmoid(pre[0:128])
-                forget = sigmoid(pre[128:256])
-                outflow = sigmoid(pre[256:384])
-                candidate = jnp.tanh(pre[384:512])
-                for n, gate in enumerate((inflow, forget, outflow, candidate)):
-                    gate_wide[pl.ds(y + n * 1024, 128, stride=8), :] = gate
                 old = cell[index, pl.ds(y, 128, stride=8), :]
-                new = forget * old + inflow * candidate
+                gates, new, state = advance(acc[:, r * 128:(r + 1) * 128], old)
+                spread_gates(gate_wide, y, gates)
                 cell[index, pl.ds(y, 128, stride=8), :] = new
-                state = outflow * jnp.tanh(new)
                 if step == 0:
                     patch[1, 1, 1 + y, slot(1 + index), :] = state.astype(BF16)
                 else:
@@ -205,12 +214,12 @@
     def finish(step, index):
         def narrow(n, carry):
             rows = pl.ds(pl.multiple_of(n * 256, 256), 256)
-            gate_narrow[step, index, rows, :] = gate_wide[rows, :].astype(BF16)
+            gate_narrow[2 * step + index * (1 - step), rows, :] = gate_wide[rows, :].astype(BF16)
             return carry
 
         lax.fori_loop(0, 16, narrow, 0, unroll=4)
         if step == 1:
-            hidden_narrow[index] = spread[...].astype(BF16)
+            hidden_narrow[...] = spread[...].astype(BF16)
 
     def start(copies):
         for copy in copies:
@@ -305,11 +314,12 @@
                 wait_recv(cross(step)[3:])
                 shift(step, 0)
 
-    take_in(0, 2)
-    take_in(0, 1)
     with phase("turn0"):
         pass_turn(outer, cross(0))
+    take_in(0, 2)
+    with phase("turn0b"):
         take_turn(inner, cross(0))
+    take_in(0, 1)
     with phase("wait_w"):
         for n in (3, 4, 5):
             loads[n].wait()
@@ -363,10 +373,10 @@
         finish(1, 1)
     rest(1)
     take_in(1, 0)
-    with phase("layer_s1_0"):
-        layer(1, 0, (0,))
     with phase("finish_s1_0"):
-        finish(1, 0)
+        for b in range(3):
+            for r in range(10):
+                window[b, r] = patch[1, b, r, slot(0), :]
 
     for step in range(2):
         for index in range(3):
@@ -377,12 +387,42 @@
         wait_send(cross(1))
 
 
-def write_out(*refs):
-    sources, targets, sem = refs[:3], refs[3:6], refs[6]
-    copies = [pltpu.make_async_copy(src, dst, sem.at[n]) for n, (src, dst) in enumerate(zip(sources, targets))]
-    for copy in copies:
+def last_layer(
+    gates, hidden_second, memory, window, partial, weight,
+    hidden_out, memory_out, gates_out,
+    gate_wide, gate_narrow, spread, hidden_narrow, cell, sem,
+):
+    def write(n, src, dst):
+        return pltpu.make_async_copy(src, dst, sem.at[n])
+
+    early = [
+        write(0, gates.at[0], gates_out.at[0, 0]),
+        write(1, gates.at[1], gates_out.at[0, 1]),
+        write(2, gates.at[2], gates_out.at[1, 1]),
+        write(3, hidden_second, hidden_out.at[1]),
+        write(4, memory.at[1], memory_out.at[1]),
+    ]
+    for copy in early:
         copy.start()
-    for copy in copies:
+    for pair in range(4):
+        acc = products(weight, lambda tap, part, y: window[tap % 3, y + tap // 3], pair, (0,)) + partial[pair]
+        for r in range(2):
+            y = 2 * pair + r
+            values, new, state = advance(acc[:, r * 128:(r + 1) * 128], memory[0, pl.ds(y, 128, stride=8), :])
+            spread_gates(gate_wide, y, values)
+            cell[pl.ds(y, 128, stride=8), :] = new
+            spread[pl.ds(y, 128, stride=8), :] = state
+    late = [write(5, cell, memory_out.at[0])]
+    late[0].start()
+    for n in range(4):
+        rows = pl.ds(n * 1024, 1024)
+        gate_narrow[rows, :] = gate_wide[rows, :].astype(BF16)
+        late.append(write(6 + n, gate_narrow.at[rows], gates_out.at[1, 0, rows]))
+        late[-1].start()
+    hidden_narrow[...] = spread[...].astype(BF16)
+    late.append(write(10, hidden_narrow, hidden_out.at[0]))
+    late[-1].start()
+    for copy in early + late:
         copy.wait()
 
 
@@ -399,19 +439,26 @@
     )
     results = pl.pallas_call(
         kernel,
-        out_shape=shapes,
+        out_shape=(
+            jax.ShapeDtypeStruct((3, 4096, 128), BF16),
+            jax.ShapeDtypeStruct((1024, 128), BF16),
+            jax.ShapeDtypeStruct((2, 1024, 128), F32),
+            jax.ShapeDtypeStruct((3, 10, 128, 128), BF16),
+            jax.ShapeDtypeStruct((4, 512, 256), F32),
+            jax.ShapeDtypeStruct((512, 2304), BF16),
+        ),
         in_specs=[pl.BlockSpec(memory_space=pltpu.HBM)] * 5,
-        out_specs=[pl.BlockSpec(memory_space=pltpu.VMEM)] * 3,
+        out_specs=[pl.BlockSpec(memory_space=pltpu.VMEM)] * 6,
         scratch_shapes=[
             vmem((2, 3, 10, 384, 128), BF16),
             vmem((1024, 128), F32),
             vmem((2, 1024, 128), BF16),
             vmem((2, 1024, 128), BF16),
-            vmem((2, 512, 2304), BF16),
+            vmem((512, 2304), BF16),
             vmem((2, 512), F32),
             vmem((2, 512, 128), F32),
             vmem((4096, 128), F32),
-            vmem((2, 4, 512, 256), F32),
+            vmem((4, 512, 256), F32),
             vmem((2, 3, 2, 8, 128), BF16),
             vmem((2, 3, 6, 8, 128), BF16),
             dma((6,)),
@@ -427,13 +474,20 @@
         name="wavefront",
     )(*[pltpu.with_memory_space_constraint(x, pltpu.HBM) for x in (frames, hidden_init, memory_init, weights, biases)])
     hidden_out, memory_out, gates_out = pl.pallas_call(
-        write_out,
+        last_layer,
         out_shape=shapes,
-        in_specs=[pl.BlockSpec(memory_space=pl.ANY)] * 3,
+        in_specs=[pl.BlockSpec(memory_space=pltpu.VMEM)] * 6,
         out_specs=[pl.BlockSpec(memory_space=pltpu.HBM)] * 3,
-        scratch_shapes=[dma((3,))],
-        compiler_params=pltpu.CompilerParams(vmem_limit_bytes=1 << 20),
-        name="write_out",
+        scratch_shapes=[
+            vmem((4096, 128), F32),
+            vmem((4096, 128), BF16),
+            vmem((1024, 128), F32),
+            vmem((1024, 128), BF16),
+            vmem((1024, 128), F32),
+            dma((11,)),
+        ],
+        compiler_params=pltpu.CompilerParams(vmem_limit_bytes=24 << 20),
+        name="last_layer",
     )(*results)
     return (
         hidden_out.reshape(2, 1, 128, 8, 128),

time: 48.5 us -> 47.5 us (0.979)
  Pallas kernels: 47.8 us -> 46.8 us
    pallas_call x2, Pallas kernels: 47.8 us -> 46.8 us  [the longest x1 43.2 us: body(): pl.pallas_call(kernel, out_shape=(jax.ShapeDtypeStruct((3, 4096, 128), BF...]
where the time goes in v4:
time: 47.5 us; the launch traced here: 47.4 us
  Pallas kernels  46.8 us (99%)
  between operations  0.64 us (1%)
    pallas_call x1, Pallas kernels, body(): pl.pallas_call(kernel, out_shape=(jax.ShapeDtypeStruct((3, 4096, 128), BF...  43.2 us
    pallas_call x1, Pallas kernels, body(): pl.pallas_call(last_layer, out_shape=shapes, in_specs=[pl.BlockSpec(memor...  3.62 us

profile of v4, /device:TPU:128, one launch (start us, length us, event | category | flops | bytes accessed | tf_op | source)
XLA Modules:
  0.0 47.4 jit_solution(2724812892682871706)
XLA Ops:
  0.6 43.2 %wavefront.1 = (bf16[3,4096,128]{2,1,0:T(8,128)(2,1)S(1)}, bf16[1024,128]{1,0:T(8,128)(2,1)S(1)}, f32[2,1024,128]{2,1,0:T(8,128)S(1)}, bf16[3,10,128,128]{3,2,1,...) custom-call(bf16[2,1024,128]{2,1,0:T(8,128)(2,1)} %bitcast.13, ...), custom_call_target="tpu_custom_call" | custom-call | tf_op jit(solution)/shard_map/wavefront/pallas_call | solution.py:440
  43.8 3.6 %last_layer.1 = (bf16[2,1024,128]{2,1,0:T(8,128)(2,1)}, f32[2,1024,128]{2,1,0:T(8,128)}, bf16[2,2,4096,128]{3,2,1,0:T(8,128)(2,1)}) custom-call(bf16[3,4096,128]{2,1,0:T(8,128)(2,1)S(1)} %get-tuple-element.12.gates, bf16[1024,128]{1,0:T(8,128)(2,1)S(1)} %get-tuple-element.13.hidden_second, f32[2,1024,128]{2,1,0:T(8,128)S(1)} %get-tuple-element.14.memory, ...), custom_call_target="tpu_custom_call" | custom-call | tf_op jit(solution)/shard_map/last_layer/pallas_call | solution.py:476
